TPU v7x, 32 devices: a whole 2x2x4 slice. The times are simulated.
32 devices in a mesh: worker: 8 (over y, x, core), mp: 4 (over z).
Axes of the slice: x: 2, y: 2, z: 4, core: 2. Of those that a mesh axis runs over, the one named last changes fastest.
Arguments:
- gradients: float32 [8, 2097152], P('worker', 'mp'), may hold values from -100 to 100
- neighbours: int32 [8, 3], replicated, may hold values from 0 to 7, as said below
- winner: int32 [1], replicated, may hold values from 0 to 7
Outputs:
- scores: float32 [8], replicated
- aggregate: float32 [2097152], P(('mp', 'worker'))
Inputs may be any that keep to these rules, and one draw needn't show every extreme that they name: `neighbours`: row i lists 3 different workers, none of them equal to i.
All inputs are finite; a program needn't handle non-finite values.
Results may differ from a plain program's by a relative error of at most 0.0003.
Values may be sent and summed in bfloat16 or wider, within the bound.
A program may use at most 64 MiB of HBM per device.

v0:
```python
import jax
import jax.numpy as jnp
from jax import lax
from jax.sharding import PartitionSpec as P


def from_root(block, axis, holder):
    block = jnp.where(lax.axis_index(axis) == holder, block, jnp.zeros_like(block))
    return lax.psum(block, axis)


def body(gradients, neighbours, winner):
    rounded = gradients.astype(jnp.bfloat16)
    workers = lax.axis_size("worker")
    own_index = lax.axis_index("worker")
    length = gradients.shape[1]
    columns = lax.all_to_all(rounded, "worker", split_axis=1, concat_axis=0, tiled=True)
    partial_value = lax.dot_general(
        columns, columns, (((1,), (1,)), ((), ())), preferred_element_type=jnp.float32
    )
    gram_matrix = lax.psum(partial_value, ("worker", "mp"))
    squares = jnp.diagonal(gram_matrix)
    distance = squares[:, None] + squares[None, :] - 2.0 * gram_matrix
    counts = jnp.sum(
        (neighbours[:, :, None] == jnp.arange(workers, dtype=jnp.int32)[None, None, :]).astype(
            jnp.float32
        ),
        axis=1,
    )
    total_entries = neighbours.shape[1] * length * lax.axis_size("mp")
    scores = jnp.sum(counts * distance, axis=1) / jnp.float32(total_entries)
    piece_length = length // workers
    selected = from_root(gradients[0], "worker", winner[0])
    aggregate = lax.dynamic_slice_in_dim(selected, own_index * piece_length, piece_length, 0)
    return (scores, aggregate)


def solution(mesh):
    in_specs = (P("worker", "mp"), P(), P())
    out_specs = (P(), P(("mp", "worker")))
    return jax.shard_map(body, mesh=mesh, in_specs=in_specs, out_specs=out_specs, check_vma=False)
```

profile of v0, /device:TPU:0, one launch (start us, length us, event | category | flops | bytes accessed | tf_op | source)
XLA Modules:
  0.0 107.3 jit_solution(818342998343869056)
XLA Ops:
  7.8 6.5 %broadcast_select_fusion = (f32[1,524288]{1,0:T(1,128)}, bf16[1,524288]{1,0:T(2,128)(2,1)S(1)}) fusion(f32[1,524288]{1,0:T(1,128)} %param.3, pred[]{:T(512)S(6)} %eq.19), kind=kLoop, calls=%fused_computation.1 | loop fusion | flops 1048576 | bytes 5242881 | tf_op jit(solution)/shard_map/jit(_where)/select_n | solution.py:8
  14.3 0.5 broadcast.34
  14.8 7.0 %reduce = bf16[8,65536]{1,0:T(8,128)(2,1)S(1)} reduce(bf16[8,1,65536]{2,1,0:T(2,128)(2,1)S(1)} %bitcast.12, bf16[]{:T(256)} %broadcast.34), dimensions={1}, to_apply=%bitcast.8.reduce_sub_computation | reduce | bytes 2097154
  21.9 1.9 %reshape.22 = bf16[8,2,32768]{2,1,0:T(2,128)(2,1)} reshape(bf16[8,65536]{1,0:T(8,128)(2,1)S(1)} %reduce) | data formatting | bytes 2097152
  23.7 0.0 copy-start
  23.7 5.3 %all-to-all-start = ((bf16[8,2,32768]{2,1,0:T(2,128)(2,1)}), bf16[8,2,32768]{2,1,0:T(2,128)(2,1)S(1)}, u32[]{:S(2)}, u32[]{:S(2)}) async-start(bf16[8,2,32768]{2,1,0:T(2,128)(2,1)} %reshape.22), calls=%async_computation | async-start | bytes 2097152 | tf_op jit(solution)/shard_map/all_to_all | solution.py:17
  29.1 0.0 all-reduce.2.cloned.1.call-start
  29.1 0.7 all-reduce.2.cloned.1.call-update
  29.8 0.0 copy-done
  29.8 0.1 convert_reduce_fusion
  29.9 16.4 %all-to-all-done = bf16[8,2,32768]{2,1,0:T(2,128)(2,1)S(1)} async-done(((bf16[8,2,32768]{2,1,0:T(2,128)(2,1)}), bf16[8,2,32768]{2,1,0:T(2,128)(2,1)S(1)}, u32[]{:S(2)}, u32[]{:S(2)}) %all-to-all-start) | async-done | bytes 1048608 | tf_op jit(solution)/shard_map/all_to_all | solution.py:17
  46.3 1.0 reshape.23
  47.3 1.2 %fusion = f32[8,8]{1,0:T(8,128)S(1)} fusion(bf16[1,8,65536]{2,0,1:T(2,128)(2,1)S(1)} %bitcast.13), kind=kOutput, calls=%fused_computation.2 | convolution fusion | flops 8388608 | bytes 1048832 | tf_op jit(solution)/shard_map/dot_general | solution.py:18
  48.5 39.8 %psum.14 = f32[8,8]{1,0:T(8,128)S(1)} all-reduce(f32[8,8]{1,0:T(8,128)S(1)} %fusion), channel_id=1, replica_groups=mesh['worker'=8,'mp'=4] {'worker','mp'}, use_global_device_ids=true, to_apply=%region_1.2 | all-reduce | flops 64 | bytes 512 | tf_op jit(solution)/shard_map/psum | solution.py:21
  88.3 0.6 gather_fusion
  88.9 0.2 multiply_reduce_fusion
  89.1 0.5 broadcast_multiply_fusion
  89.6 9.1 %all-reduce.2.cloned.1.call-done = f32[524288]{0:T(1024)} async-done(((f32[524288]{0:T(1024)}), f32[524288]{0:T(1024)}) %all-reduce.2.cloned.1.call-update) | async-done | bytes 2097168 | tf_op jit(solution)/shard_map/psum | solution.py:9
  98.8 1.7 %dynamic_slice.3 = f32[65536]{0:T(1024)} dynamic-slice(f32[524288]{0:T(1024)} %all-reduce.2.cloned.1.call-done, s32[]{:T(128)S(6)} %select_n.21), dynamic_slice_sizes={65536} | dynamic-slice | bytes 524292 | tf_op jit(solution)/shard_map/dynamic_slice | solution.py:34
  (1 shorter events, 0.0 us)
Async XLA Ops:
  23.7 6.1 %copy-start = (s32[8,3]{0,1:T(4,128)S(1)}, s32[8,3]{0,1:T(4,128)}, u32[]{:S(2)}) copy-start(s32[8,3]{0,1:T(4,128)} %param.4) | copy-start | bytes 292
  23.7 22.5 %all-to-all-start = ((bf16[8,2,32768]{2,1,0:T(2,128)(2,1)}), bf16[8,2,32768]{2,1,0:T(2,128)(2,1)S(1)}, u32[]{:S(2)}, u32[]{:S(2)}) async-start(bf16[8,2,32768]{2,1,0:T(2,128)(2,1)} %reshape.22), calls=%async_computation | async-start | bytes 2097152 | tf_op jit(solution)/shard_map/all_to_all | solution.py:17
  29.1 69.7 %all-reduce.2.cloned.1.call-start = ((), (), s32[]{:S(2)}) async-start(), calls=%async_computation.1 | async-start | bytes 4194304 | tf_op jit(solution)/shard_map/psum | solution.py:9
Sparse Core Ops, SparseCore 0:
  33.1 65.6 all-reduce.1
where the time goes:
time: 108 us; the launch traced here: 107 us
  blocking collectives  39.8 us (37%)
  waiting for transfers between devices  26.2 us (24%)
  between operations  14.7 us (14%)
  other arithmetic  14.3 us (13%)
  local copies, waits for them, and re-layouts  5.71 us (5%)
  starting transfers between devices  5.37 us (5%)
  matrix products  1.2 us (1%)
    psum x1, blocking collectives, body(): gram_matrix = lax.psum(partial_value, ('worker', 'mp'))  39.8 us
    all_to_all x1, waiting for transfers between devices, body(): lax.all_to_all(rounded, 'worker', split_axis=1, concat_axis=0, tiled=True)  16.4 us
    psum x1, waiting for transfers between devices, from_root(): return lax.psum(block, axis)  9.12 us
    unnamed x1, other arithmetic  7.03 us
    select_n x1, other arithmetic, from_root(): jnp.where(lax.axis_index(axis) == holder, block, jnp.zeros_like(block))  6.5 us
    all_to_all x1, starting transfers between devices, body(): lax.all_to_all(rounded, 'worker', split_axis=1, concat_axis=0, tiled=True)  5.33 us
    unnamed x5, local copies, waits for them, and re-layouts  3.41 us
  transfers between devices with their start and end apart: 2, of which 2 were waited for; matrix products, arithmetic and copies ran while one was open for 3% of the time, Pallas kernels for 0%

commit v1 on v0

v1 whole, which is shorter than its diff:
```python
import functools

import jax
import jax.numpy as jnp
from jax import lax
from jax.experimental import pallas as pl
from jax.experimental.pallas import tpu as pltpu
from jax.sharding import PartitionSpec as P

MESH = pl.DeviceIdType.MESH
LANES = 128
CHUNKS = 4


def flip(index, offset, size):
    result, bit = 0, 1
    while bit < size:
        digit = (index // bit) % 2
        if (offset // bit) % 2:
            digit = 1 - digit
        result = result + digit * bit
        bit *= 2
    return result


def kernel(
    workers,
    planes,
    total_entries,
    nb_ref,
    win_ref,
    g_ref,
    scores_ref,
    out_ref,
    stage,
    rounded,
    recv,
    rest,
    rest_in,
    rest_recv,
    dist,
    part,
    zbuf,
    plane_part,
    pbuf,
    load_sem,
    gsend,
    grecv,
    osend,
    orecv,
    rsend,
    rrecv,
    zsend,
    zrecv,
    psend,
    precv,
):
    me = lax.axis_index("worker")
    plane = lax.axis_index("mp")
    core = me % 2
    chip = me // 2
    chips = workers // 2
    rows = stage.shape[1]
    span = rows // CHUNKS
    order = sorted(range(2, workers), key=lambda o: (bin(o // 2).count("1"), o % 2, o)) + [1, 0]
    near = [o for o in range(1, workers) if bin(o // 2).count("1") < 2]
    far = [o for o in order if bin(o // 2).count("1") >= 2]
    peer = [flip(me, o, workers) for o in range(workers)]

    barrier = pltpu.get_barrier_semaphore()
    for o in range(1, workers):
        pl.semaphore_signal(barrier, inc=1, device_id={"worker": peer[o]}, device_id_type=MESH)
    for z in range(1, planes):
        pl.semaphore_signal(
            barrier, inc=1, device_id={"mp": (plane + z) % planes}, device_id_type=MESH
        )

    def load(o):
        first = pl.multiple_of(peer[o] * rows, rows)
        return pltpu.make_async_copy(g_ref.at[pl.ds(first, rows), :], stage.at[o], load_sem.at[o])

    for o in order:
        load(o).start()

    def gram_copy(o, c, slot):
        at = pl.ds(c * span, span)
        return pltpu.make_async_remote_copy(
            src_ref=rounded.at[o, at, :],
            dst_ref=recv.at[slot, at, :],
            send_sem=gsend.at[o, c],
            recv_sem=grecv.at[o, c],
            device_id={"worker": peer[o]},
            device_id_type=MESH,
        )

    def whole_copy(o, slot):
        return pltpu.make_async_remote_copy(
            src_ref=rounded.at[o],
            dst_ref=recv.at[slot],
            send_sem=gsend.at[o, 0],
            recv_sem=grecv.at[o, 0],
            device_id={"worker": peer[o]},
            device_id_type=MESH,
        )

    keep = jnp.where(win_ref[0] == me, 1.0, 0.0).astype(jnp.float32)
    block = 128

    def convert(o):
        parity = peer[o] % 2
        where = peer[o] // 2

        def one(step, carry):
            at = pl.ds(pl.multiple_of(step * block, block), block)
            x = stage[o, at, :]
            hi = x.astype(jnp.bfloat16)
            if o == 0:
                recv[me, at, :] = hi
            else:
                rounded[o, at, :] = hi
            rest[parity, where, at, :] = ((x - hi.astype(jnp.float32)) * keep).astype(jnp.bfloat16)
            return carry

        lax.fori_loop(0, rows // block, one, 0)

    for n, o in enumerate(order):
        load(o).wait()
        convert(o)
        if n == 0:
            pl.semaphore_wait(barrier, workers - 1 + planes - 1)
        if o in near:
            whole_copy(o, me).start()
        elif o in far and o % 2 == 1:
            for c in range(CHUNKS):
                gram_copy(o - 1, c, me).start()
                gram_copy(o, c, me).start()

    swap = pltpu.make_async_remote_copy(
        src_ref=rest.at[1 - core],
        dst_ref=rest_in,
        send_sem=osend,
        recv_sem=orecv,
        device_id={"worker": peer[1]},
        device_id_type=MESH,
    )
    swap.start()
    swap.wait_recv()

    def combine(step, carry):
        at = pl.ds(pl.multiple_of(step * block, block), block)
        for q in range(chips):
            rest_in[q, at, :] = rest_in[q, at, :] + rest[core, q, at, :]
        return carry

    lax.fori_loop(0, rows // block, combine, 0)

    def rest_copy(ox):
        return pltpu.make_async_remote_copy(
            src_ref=rest_in.at[flip(chip, ox, chips)],
            dst_ref=rest_recv.at[ox],
            send_sem=rsend.at[ox],
            recv_sem=rrecv.at[ox],
            device_id={"worker": peer[2 * ox]},
            device_id_type=MESH,
        )

    rest_order = sorted(range(1, chips), key=lambda ox: bin(ox).count("1"))

    pairs = [(i, k) for i in range(workers) for k in range(i, workers)]

    def gram(first, accs):
        def one(step, accs):
            at = pl.ds(pl.multiple_of(first + step * 16, 16), 16)
            xs = [recv[i, at, :].astype(jnp.float32) for i in range(workers)]
            lo = [x[:8] for x in xs]
            hi = [x[8:] for x in xs]
            return tuple(
                a + (lo[i] * lo[k] + hi[i] * hi[k]) for a, (i, k) in zip(accs, pairs)
            )

        return lax.fori_loop(0, span // 16, one, accs)

    accs = tuple(jnp.zeros((8, LANES), jnp.float32) for _ in pairs)
    for o in near:
        whole_copy(o, peer[o]).wait_recv()
    for c in range(CHUNKS):
        if c == CHUNKS - 1:
            for ox in rest_order:
                rest_copy(ox).start()
        for o in far:
            gram_copy(o, c, peer[o]).wait_recv()
        accs = gram(c * span, accs)

    value = dict(zip(pairs, accs))
    for i, k in pairs:
        if i == k:
            dist[i * workers + i] = jnp.zeros((8, LANES), jnp.float32)
        else:
            d = value[i, i] + value[k, k] - 2.0 * value[i, k]
            dist[i * workers + k] = d
            dist[k * workers + i] = d
    for i in range(workers):
        s = dist[i * workers + nb_ref[i, 0]]
        for j in range(1, nb_ref.shape[1]):
            s = s + dist[i * workers + nb_ref[i, j]]
        part[pl.ds(i, 1), :] = jnp.sum(s, axis=0, keepdims=True)

    def z_copy(z):
        return pltpu.make_async_remote_copy(
            src_ref=part,
            dst_ref=zbuf.at[z],
            send_sem=zsend.at[z],
            recv_sem=zrecv.at[z],
            device_id={"mp": (plane + z) % planes},
            device_id_type=MESH,
        )

    def p_copy(o):
        return pltpu.make_async_remote_copy(
            src_ref=plane_part,
            dst_ref=pbuf.at[o],
            send_sem=psend.at[o],
            recv_sem=precv.at[o],
            device_id={"worker": peer[o]},
            device_id_type=MESH,
        )

    for z in range(1, planes):
        z_copy(z).start()
    total = part[...]
    for z in range(1, planes):
        z_copy(z).wait_recv()
        total = total + zbuf[z]
    plane_part[...] = total
    for o in range(1, workers):
        p_copy(o).start()

    for ox in rest_order:
        rest_copy(ox).wait_recv()

    def finish(step, carry):
        at = pl.ds(pl.multiple_of(step * block, block), block)
        low = rest_in[chip, at, :].astype(jnp.float32)
        for ox in rest_order:
            low = low + rest_recv[ox, at, :].astype(jnp.float32)
        out_ref[at, :] = recv[win_ref[0], at, :].astype(jnp.float32) + low
        return carry

    lax.fori_loop(0, rows // block, finish, 0)

    for o in range(1, workers):
        p_copy(o).wait_recv()
        total = total + pbuf[o]
    column = jnp.sum(total, axis=1, keepdims=True) / jnp.float32(total_entries)
    line = lax.broadcasted_iota(jnp.int32, (workers, LANES), 0)
    lane = lax.broadcasted_iota(jnp.int32, (workers, LANES), 1)
    scores_ref[...] = jnp.sum(
        jnp.where(line == lane, column, 0.0), axis=0, keepdims=True
    )[:, :workers]

    swap.wait_send()
    for o in near:
        whole_copy(o, me).wait_send()
    for o in far:
        for c in range(CHUNKS):
            gram_copy(o, c, me).wait_send()
    for ox in rest_order:
        rest_copy(ox).wait_send()
    for z in range(1, planes):
        z_copy(z).wait_send()
    for o in range(1, workers):
        p_copy(o).wait_send()


def solution(mesh):
    workers = mesh.shape["worker"]
    planes = mesh.shape["mp"]
    chips = workers // 2

    def body(gradients, neighbours, winner):
        length = gradients.shape[1]
        rows = length // (LANES * workers)
        entries = neighbours.shape[1] * length * planes
        bf16, f32 = jnp.bfloat16, jnp.float32
        dma = pltpu.SemaphoreType.DMA
        scores, aggregate = pl.pallas_call(
            functools.partial(kernel, workers, planes, entries),
            out_shape=(
                jax.ShapeDtypeStruct((1, workers), f32),
                jax.ShapeDtypeStruct((rows, LANES), f32),
            ),
            in_specs=[
                pl.BlockSpec(memory_space=pltpu.SMEM),
                pl.BlockSpec(memory_space=pltpu.SMEM),
                pl.BlockSpec(memory_space=pl.ANY),
            ],
            out_specs=(
                pl.BlockSpec(memory_space=pltpu.VMEM),
                pl.BlockSpec(memory_space=pltpu.VMEM),
            ),
            scratch_shapes=[
                pltpu.VMEM((workers, rows, LANES), f32),
                pltpu.VMEM((workers, rows, LANES), bf16),
                pltpu.VMEM((workers, rows, LANES), bf16),
                pltpu.VMEM((2, chips, rows, LANES), bf16),
                pltpu.VMEM((chips, rows, LANES), bf16),
                pltpu.VMEM((chips, rows, LANES), bf16),
                pltpu.VMEM((workers * workers, 8, LANES), f32),
                pltpu.VMEM((workers, LANES), f32),
                pltpu.VMEM((planes, workers, LANES), f32),
                pltpu.VMEM((workers, LANES), f32),
                pltpu.VMEM((workers, workers, LANES), f32),
                dma((workers,)),
                dma((workers, CHUNKS)),
                dma((workers, CHUNKS)),
                dma,
                dma,
                dma((chips,)),
                dma((chips,)),
                dma((planes,)),
                dma((planes,)),
                dma((workers,)),
                dma((workers,)),
            ],
            compiler_params=pltpu.CompilerParams(collective_id=0, has_side_effects=True),
        )(neighbours, winner, gradients.reshape(length // LANES, LANES))
        return scores.reshape(workers), aggregate.reshape(rows * LANES)

    in_specs = (P("worker", "mp"), P(), P())
    out_specs = (P(), P(("mp", "worker")))
    return jax.shard_map(body, mesh=mesh, in_specs=in_specs, out_specs=out_specs, check_vma=False)
```

time: 108 us -> 34.1 us (0.32)
  blocking collectives: 39.8 us -> 0 us
  Pallas kernels: 0 us -> 28.5 us
  waiting for transfers between devices: 26.2 us -> 0 us
  other arithmetic: 14.3 us -> 0 us
  between operations: 14.7 us -> 1.29 us
  starting transfers between devices: 5.37 us -> 0 us
  local copies, waits for them, and re-layouts: 5.71 us -> 4.15 us
  matrix products: 1.2 us -> 0 us
    psum x1 -> x0, blocking collectives: 39.8 us -> none  [body(): gram_matrix = lax.psum(partial_value, ('worker', 'mp'))]
    pallas_call x0 -> x1, Pallas kernels: none -> 28.5 us  [body(): pl.pallas_call(functools.partial(kernel, workers, planes, entries), out_s...]
    all_to_all x1 -> x0, waiting for transfers between devices: 16.4 us -> none  [body(): lax.all_to_all(rounded, 'worker', split_axis=1, concat_axis=0, tiled=True)]
    psum x1 -> x0, waiting for transfers between devices: 9.12 us -> none  [from_root(): return lax.psum(block, axis)]
    unnamed x1 -> x0, other arithmetic: 7.03 us -> none
    select_n x1 -> x0, other arithmetic: 6.5 us -> none  [from_root(): jnp.where(lax.axis_index(axis) == holder, block, jnp.zeros_like(block))]
    all_to_all x1 -> x0, starting transfers between devices: 5.33 us -> none  [body(): lax.all_to_all(rounded, 'worker', split_axis=1, concat_axis=0, tiled=True)]
    dynamic_slice x1 -> x0, local copies, waits for them, and re-layouts: 1.67 us -> none  [body(): lax.dynamic_slice_in_dim(selected, own_index * piece_length, piece_length...]
  transfers between devices with their start and end apart: 2 -> 0, of which waited for: 2 -> 0; matrix products, arithmetic and copies ran while one was open for 3% -> 0% of each run, Pallas kernels for 0% -> 0%
where the time goes in v1:
time: 34.1 us; the launch traced here: 33.9 us
  Pallas kernels  28.5 us (84%)
  local copies, waits for them, and re-layouts  4.15 us (12%)
  between operations  1.29 us (4%)
    pallas_call x1, Pallas kernels, body(): pl.pallas_call(functools.partial(kernel, workers, planes, entries), out_s...  28.5 us
    unnamed x3, local copies, waits for them, and re-layouts  4.15 us

profile of v1, /device:TPU:0, one launch (start us, length us, event | category | flops | bytes accessed | tf_op | source)
XLA Modules:
  0.0 33.9 jit_solution(8449922086300285597)
XLA Ops:
  1.3 1.3 %copy.5.nb_ref = s32[8,3]{1,0:T(8,128)} copy(s32[8,3]{0,1:T(4,128)} %param.4) | data formatting | bytes 192 | tf_op args[1]
  2.6 28.5 %shard_map.50 = (f32[1,8]{1,0:T(1,128)}, f32[512,128]{1,0:T(8,128)}) custom-call(s32[8,3]{1,0:T(8,128)} %copy.5.nb_ref, s32[1]{0:T(128)S(6)} %copy.8.win_ref, f32[4096,128]{1,0:T(8,128)} %bitcast.3), custom_call_target="tpu_custom_call" | custom-call | tf_op jit(solution)/shard_map/pallas_call | solution.py:286
  31.1 1.1 %copy.9 = f32[8]{0:T(128)} copy(f32[8]{0:T(128)} %bitcast.5) | data formatting | bytes 64
  32.2 1.7 %copy.10 = f32[65536]{0:T(1024)} copy(f32[65536]{0:T(1024)} %bitcast.4) | data formatting | bytes 524288

commit v2 on v1

--- a/solution.py
+++ b/solution.py
@@ -27,27 +27,32 @@
     workers,
     planes,
     total_entries,
-    nb_ref,
+    nb_hbm,
     win_ref,
     g_ref,
     scores_ref,
     out_ref,
+    nb_ref,
     stage,
     rounded,
     recv,
     rest,
     rest_in,
     rest_recv,
+    relay,
     dist,
     part,
     zbuf,
     plane_part,
     pbuf,
+    small_sem,
     load_sem,
     gsend,
     grecv,
     osend,
     orecv,
+    ysend,
+    yrecv,
     rsend,
     rrecv,
     zsend,
@@ -79,7 +84,10 @@
         first = pl.multiple_of(peer[o] * rows, rows)
         return pltpu.make_async_copy(g_ref.at[pl.ds(first, rows), :], stage.at[o], load_sem.at[o])
 
-    for o in order:
+    lists = pltpu.make_async_copy(nb_hbm, nb_ref, small_sem)
+    load(order[0]).start()
+    lists.start()
+    for o in order[1:]:
         load(o).start()
 
     def gram_copy(o, c, slot):
@@ -123,6 +131,43 @@
 
         lax.fori_loop(0, rows // block, one, 0)
 
+    def swap(ox):
+        there = flip(chip, ox, chips)
+        return pltpu.make_async_remote_copy(
+            src_ref=rest.at[1 - core, there],
+            dst_ref=rest_in.at[there],
+            send_sem=osend.at[ox],
+            recv_sem=orecv.at[ox],
+            device_id={"worker": peer[1]},
+            device_id_type=MESH,
+        )
+
+    def add_to_rest(there, first, count, other):
+        def one(step, carry):
+            at = pl.ds(pl.multiple_of(first + step * block, block), block)
+            rest_in[there, at, :] = rest_in[there, at, :] + other(at)
+            return carry
+
+        lax.fori_loop(0, count // block, one, 0)
+
+    def combine(ox):
+        there = flip(chip, ox, chips)
+        swap(ox).wait_recv()
+        add_to_rest(there, 0, rows, lambda at: rest[core, there, at, :])
+
+    split = chips == 4
+    half = rows // 2
+
+    def relay_copy(ox):
+        return pltpu.make_async_remote_copy(
+            src_ref=rest_in.at[flip(chip, 3, chips), pl.ds((ox - 1) * half, half), :],
+            dst_ref=relay.at[ox - 1],
+            send_sem=ysend.at[ox - 1],
+            recv_sem=yrecv.at[ox - 1],
+            device_id={"worker": peer[2 * ox]},
+            device_id_type=MESH,
+        )
+
     for n, o in enumerate(order):
         load(o).wait()
         convert(o)
@@ -130,29 +175,20 @@
             pl.semaphore_wait(barrier, workers - 1 + planes - 1)
         if o in near:
             whole_copy(o, me).start()
-        elif o in far and o % 2 == 1:
-            for c in range(CHUNKS):
-                gram_copy(o - 1, c, me).start()
-                gram_copy(o, c, me).start()
-
-    swap = pltpu.make_async_remote_copy(
-        src_ref=rest.at[1 - core],
-        dst_ref=rest_in,
-        send_sem=osend,
-        recv_sem=orecv,
-        device_id={"worker": peer[1]},
-        device_id_type=MESH,
-    )
-    swap.start()
-    swap.wait_recv()
-
-    def combine(step, carry):
-        at = pl.ds(pl.multiple_of(step * block, block), block)
-        for q in range(chips):
-            rest_in[q, at, :] = rest_in[q, at, :] + rest[core, q, at, :]
-        return carry
-
-    lax.fori_loop(0, rows // block, combine, 0)
+        if o % 2 == 1:
+            swap(o // 2).start()
+
+    if split:
+        combine(3)
+        relay_copy(1).start()
+        relay_copy(2).start()
+    for o in far[::2]:
+        for c in range(CHUNKS):
+            gram_copy(o, c, me).start()
+            gram_copy(o + 1, c, me).start()
+    for ox in range(chips):
+        if not (split and ox == 3):
+            combine(ox)
 
     def rest_copy(ox):
         return pltpu.make_async_remote_copy(
@@ -165,6 +201,8 @@
         )
 
     rest_order = sorted(range(1, chips), key=lambda ox: bin(ox).count("1"))
+    if split:
+        rest_order = [1, 2]
 
     pairs = [(i, k) for i in range(workers) for k in range(i, workers)]
 
@@ -184,7 +222,19 @@
     for o in near:
         whole_copy(o, peer[o]).wait_recv()
     for c in range(CHUNKS):
-        if c == CHUNKS - 1:
+        if c == CHUNKS - 2:
+            for ox in rest_order:
+                if split:
+                    first = (ox - 1) * half
+                    relay_copy(ox).wait_recv()
+                    add_to_rest(
+                        flip(chip, 3 - ox, chips),
+                        first,
+                        half,
+                        lambda at, first=first, ox=ox: relay[
+                            ox - 1, pl.ds(pl.multiple_of(at.start - first, block), block), :
+                        ],
+                    )
             for ox in rest_order:
                 rest_copy(ox).start()
         for o in far:
@@ -199,10 +249,11 @@
             d = value[i, i] + value[k, k] - 2.0 * value[i, k]
             dist[i * workers + k] = d
             dist[k * workers + i] = d
+    lists.wait()
     for i in range(workers):
-        s = dist[i * workers + nb_ref[i, 0]]
-        for j in range(1, nb_ref.shape[1]):
-            s = s + dist[i * workers + nb_ref[i, j]]
+        s = dist[i * workers + nb_ref[0, i]]
+        for j in range(1, nb_ref.shape[0]):
+            s = s + dist[i * workers + nb_ref[j, i]]
         part[pl.ds(i, 1), :] = jnp.sum(s, axis=0, keepdims=True)
 
     def z_copy(z):
@@ -258,7 +309,11 @@
         jnp.where(line == lane, column, 0.0), axis=0, keepdims=True
     )[:, :workers]
 
-    swap.wait_send()
+    for ox in range(chips):
+        swap(ox).wait_send()
+    if split:
+        relay_copy(1).wait_send()
+        relay_copy(2).wait_send()
     for o in near:
         whole_copy(o, me).wait_send()
     for o in far:
@@ -272,6 +327,17 @@
         p_copy(o).wait_send()
 
 
+def emit(scores_ref, block_ref, scores_out, block_out, sems):
+    copies = [
+        pltpu.make_async_copy(block_ref, block_out, sems.at[0]),
+        pltpu.make_async_copy(scores_ref, scores_out, sems.at[1]),
+    ]
+    for copy in copies:
+        copy.start()
+    for copy in copies:
+        copy.wait()
+
+
 def solution(mesh):
     workers = mesh.shape["worker"]
     planes = mesh.shape["mp"]
@@ -286,35 +352,40 @@
         scores, aggregate = pl.pallas_call(
             functools.partial(kernel, workers, planes, entries),
             out_shape=(
-                jax.ShapeDtypeStruct((1, workers), f32),
-                jax.ShapeDtypeStruct((rows, LANES), f32),
+                pltpu.VMEM((1, workers), f32),
+                pltpu.VMEM((rows, LANES), f32),
             ),
             in_specs=[
+                pl.BlockSpec(memory_space=pltpu.HBM),
                 pl.BlockSpec(memory_space=pltpu.SMEM),
-                pl.BlockSpec(memory_space=pltpu.SMEM),
-                pl.BlockSpec(memory_space=pl.ANY),
+                pl.BlockSpec(memory_space=pltpu.HBM),
             ],
             out_specs=(
                 pl.BlockSpec(memory_space=pltpu.VMEM),
                 pl.BlockSpec(memory_space=pltpu.VMEM),
             ),
             scratch_shapes=[
+                pltpu.SMEM(neighbours.shape[::-1], jnp.int32),
                 pltpu.VMEM((workers, rows, LANES), f32),
                 pltpu.VMEM((workers, rows, LANES), bf16),
                 pltpu.VMEM((workers, rows, LANES), bf16),
                 pltpu.VMEM((2, chips, rows, LANES), bf16),
                 pltpu.VMEM((chips, rows, LANES), bf16),
                 pltpu.VMEM((chips, rows, LANES), bf16),
+                pltpu.VMEM((2, rows // 2, LANES), bf16),
                 pltpu.VMEM((workers * workers, 8, LANES), f32),
                 pltpu.VMEM((workers, LANES), f32),
                 pltpu.VMEM((planes, workers, LANES), f32),
                 pltpu.VMEM((workers, LANES), f32),
                 pltpu.VMEM((workers, workers, LANES), f32),
+                dma,
                 dma((workers,)),
                 dma((workers, CHUNKS)),
                 dma((workers, CHUNKS)),
-                dma,
-                dma,
+                dma((chips,)),
+                dma((chips,)),
+                dma((2,)),
+                dma((2,)),
                 dma((chips,)),
                 dma((chips,)),
                 dma((planes,)),
@@ -322,8 +393,21 @@
                 dma((workers,)),
                 dma((workers,)),
             ],
-            compiler_params=pltpu.CompilerParams(collective_id=0, has_side_effects=True),
-        )(neighbours, winner, gradients.reshape(length // LANES, LANES))
+            compiler_params=pltpu.CompilerParams(
+                collective_id=0, has_side_effects=True, vmem_limit_bytes=63_500_000
+            ),
+        )(neighbours.T, winner, gradients.reshape(length // LANES, LANES))
+        scores, aggregate = pl.pallas_call(
+            emit,
+            out_shape=(
+                jax.ShapeDtypeStruct(scores.shape, f32),
+                jax.ShapeDtypeStruct(aggregate.shape, f32),
+            ),
+            in_specs=[pl.BlockSpec(memory_space=pltpu.VMEM)] * 2,
+            out_specs=(pl.BlockSpec(memory_space=pl.ANY),) * 2,
+            scratch_shapes=[dma((2,))],
+            compiler_params=pltpu.CompilerParams(vmem_limit_bytes=8 * 1024 * 1024),
+        )(scores, aggregate)
         return scores.reshape(workers), aggregate.reshape(rows * LANES)
 
     in_specs = (P("worker", "mp"), P(), P())

time: 34.1 us -> 30.7 us (0.900)
  local copies, waits for them, and re-layouts: 4.15 us -> 0 us
  Pallas kernels: 28.5 us -> 29.3 us
    unnamed x3 -> x0, local copies, waits for them, and re-layouts: 4.15 us -> none
    pallas_call x0 -> x1, Pallas kernels: none -> 0.72 us  [body(): pl.pallas_call(emit, out_shape=(jax.ShapeDtypeStruct(scores.shape, f32),...]
where the time goes in v2:
time: 30.7 us; the launch traced here: 30.6 us
  Pallas kernels  29.3 us (95%)
  between operations  1.28 us (4%)
    pallas_call x1, Pallas kernels, body(): pl.pallas_call(functools.partial(kernel, workers, planes, entries), out_s...  28.6 us
    pallas_call x1, Pallas kernels, body(): pl.pallas_call(emit, out_shape=(jax.ShapeDtypeStruct(scores.shape, f32),...  0.72 us

profile of v2, /device:TPU:0, one launch (start us, length us, event | category | flops | bytes accessed | tf_op | source)
XLA Modules:
  0.0 30.6 jit_solution(9690532765980320936)
XLA Ops:
  1.3 28.6 %shard_map.50 = (f32[1,8]{1,0:T(1,128)S(1)}, f32[512,128]{1,0:T(8,128)S(1)}) custom-call(s32[3,8]{1,0:T(4,128)} %bitcast.5, s32[1]{0:T(128)S(6)} %copy.5.win_ref, f32[4096,128]{1,0:T(8,128)} %bitcast.4), custom_call_target="tpu_custom_call" | custom-call | tf_op jit(solution)/shard_map/pallas_call | solution.py:352
  29.8 0.7 %shard_map.51 = (f32[1,8]{1,0:T(1,128)}, f32[512,128]{1,0:T(8,128)}) custom-call(f32[1,8]{1,0:T(1,128)S(1)} %get-tuple-element.6.scores_ref, f32[512,128]{1,0:T(8,128)S(1)} %get-tuple-element.7.block_ref), custom_call_target="tpu_custom_call" | custom-call | tf_op jit(solution)/shard_map/pallas_call | solution.py:400

commit v3 on v2

--- a/solution.py
+++ b/solution.py
@@ -178,14 +178,14 @@
         if o % 2 == 1:
             swap(o // 2).start()
 
+    for o in far[::2]:
+        for c in range(CHUNKS):
+            gram_copy(o, c, me).start()
+            gram_copy(o + 1, c, me).start()
     if split:
         combine(3)
         relay_copy(1).start()
         relay_copy(2).start()
-    for o in far[::2]:
-        for c in range(CHUNKS):
-            gram_copy(o, c, me).start()
-            gram_copy(o + 1, c, me).start()
     for ox in range(chips):
         if not (split and ox == 3):
             combine(ox)
@@ -222,21 +222,6 @@
     for o in near:
         whole_copy(o, peer[o]).wait_recv()
     for c in range(CHUNKS):
-        if c == CHUNKS - 2:
-            for ox in rest_order:
-                if split:
-                    first = (ox - 1) * half
-                    relay_copy(ox).wait_recv()
-                    add_to_rest(
-                        flip(chip, 3 - ox, chips),
-                        first,
-                        half,
-                        lambda at, first=first, ox=ox: relay[
-                            ox - 1, pl.ds(pl.multiple_of(at.start - first, block), block), :
-                        ],
-                    )
-            for ox in rest_order:
-                rest_copy(ox).start()
         for o in far:
             gram_copy(o, c, peer[o]).wait_recv()
         accs = gram(c * span, accs)
@@ -278,6 +263,20 @@
 
     for z in range(1, planes):
         z_copy(z).start()
+    for ox in rest_order:
+        if split:
+            first = (ox - 1) * half
+            relay_copy(ox).wait_recv()
+            add_to_rest(
+                flip(chip, 3 - ox, chips),
+                first,
+                half,
+                lambda at, first=first, ox=ox: relay[
+                    ox - 1, pl.ds(pl.multiple_of(at.start - first, block), block), :
+                ],
+            )
+    for ox in rest_order:
+        rest_copy(ox).start()
     total = part[...]
     for z in range(1, planes):
         z_copy(z).wait_recv()

time: 30.7 us -> 29.6 us (0.964)
  Pallas kernels: 29.3 us -> 28.1 us
    pallas_call x1, Pallas kernels: 28.6 us -> 27.4 us  [body(): pl.pallas_call(functools.partial(kernel, workers, planes, entries), out_s...]
where the time goes in v3:
time: 29.6 us; the launch traced here: 29.4 us
  Pallas kernels  28.1 us (95%)
  between operations  1.28 us (4%)
    pallas_call x1, Pallas kernels, body(): pl.pallas_call(functools.partial(kernel, workers, planes, entries), out_s...  27.4 us
    pallas_call x1, Pallas kernels, body(): pl.pallas_call(emit, out_shape=(jax.ShapeDtypeStruct(scores.shape, f32),...  0.72 us

profile of v3, /device:TPU:0, one launch (start us, length us, event | category | flops | bytes accessed | tf_op | source)
XLA Modules:
  0.0 29.4 jit_solution(5601970575656383911)
XLA Ops:
  1.3 27.4 %shard_map.50 = (f32[1,8]{1,0:T(1,128)S(1)}, f32[512,128]{1,0:T(8,128)S(1)}) custom-call(s32[3,8]{1,0:T(4,128)} %bitcast.5, s32[1]{0:T(128)S(6)} %copy.5.win_ref, f32[4096,128]{1,0:T(8,128)} %bitcast.4), custom_call_target="tpu_custom_call" | custom-call | tf_op jit(solution)/shard_map/pallas_call | solution.py:351
  28.7 0.7 %shard_map.51 = (f32[1,8]{1,0:T(1,128)}, f32[512,128]{1,0:T(8,128)}) custom-call(f32[1,8]{1,0:T(1,128)S(1)} %get-tuple-element.6.scores_ref, f32[512,128]{1,0:T(8,128)S(1)} %get-tuple-element.7.block_ref), custom_call_target="tpu_custom_call" | custom-call | tf_op jit(solution)/shard_map/pallas_call | solution.py:399
